TPU v7x, 32 devices: a whole 2x2x4 slice. The times are simulated.
32 devices in a mesh: patch: 16 (over z, y, x), batch: 2 (over core).
Axes of the slice: x: 2, y: 2, z: 4, core: 2. Of those that a mesh axis runs over, the one named last changes fastest.
Arguments:
- tokens: bfloat16 [4096, 1152], P(('batch', 'patch')), parts along dimension 0, may hold values from -6 to 6
- slots: int32 [4096], P(('batch', 'patch')), parts along dimension 0, may hold values from 0 to 127, as said below
- counts: int32 [32], P(('batch', 'patch')), parts along dimension 0, may hold values from 32 to 128, as said below
- shift: float32 [1152], replicated, may hold values from -3 to 3
- scale: float32 [1152], replicated, may hold values from -3 to 3
- gate: float32 [1152], replicated, may hold values from -4 to 4
- w_qkv: bfloat16 [1152, 3456], replicated, may hold values from -1 to 1
- w_out: bfloat16 [1152, 1152], replicated, may hold values from -0.1875 to 0.1875
Outputs:
- result: bfloat16 [4096, 1152], P(('batch', 'patch')), parts along dimension 0
There are 2 independent parts, one for each index of `batch`. A program takes and returns all parts, laid end to end along the dimension named above; an argument that names none is the same for every part. Nothing has to cross between parts.
Inputs may be any that keep to these rules, and one draw needn't show every extreme that they name: `counts`: at least a quarter of each block's slots are live. The live slots of all blocks of an image number exactly 80 times the number of patch devices, and all blocks of some device are full. `slots`: every token's slot is below its block's count, and every slot below the count holds at least one token.
All inputs are finite; a program needn't handle non-finite values.
Results may differ from a plain program's by a relative error of at most 0.011.
Values may be sent and summed in bfloat16 or wider, within the bound.
A program may use at most 192 MiB of HBM per device.

v0:
```python
import jax
import jax.numpy as jnp
from jax import lax
from jax.sharding import PartitionSpec as P

HEADS = 16
BLK = 128


def layer_norm(merged, shift, scale):
    values = merged.astype(jnp.float32)
    center = jnp.mean(values, axis=-1, keepdims=True)
    spread = jnp.mean((values - center) ** 2, axis=-1, keepdims=True)
    return ((values - center) * lax.rsqrt(spread + 1e-06) * (1.0 + scale) + shift).astype(
        jnp.bfloat16
    )


def size_bias(sizes):
    return jnp.log(jnp.maximum(sizes.astype(jnp.float32), 1.0))


def empty_carry(heads, query_rows, head_size):
    return (
        jnp.full((heads, query_rows), -1e30, jnp.float32),
        jnp.zeros((heads, query_rows), jnp.float32),
        jnp.zeros((heads, query_rows, head_size), jnp.float32),
    )


def finish(accum, total):
    heads, query_rows, head_size = accum.shape
    return (
        (accum / total[:, :, None])
        .transpose(1, 0, 2)
        .reshape(query_rows, heads * head_size)
        .astype(jnp.bfloat16)
    )


def attend_piece(query, carry, keys, values, bias, inverse):
    top, total, accum = carry
    key_rows = keys.shape[0]
    heads = query.shape[1]
    key_heads = keys.reshape(key_rows, heads, -1)
    value_heads = values.reshape(key_rows, heads, -1)
    score = (
        jnp.einsum("qhe,khe->hqk", query, key_heads, preferred_element_type=jnp.float32) * inverse
        + bias[None, None, :]
    )
    new_top = jnp.maximum(top, jnp.max(score, axis=-1))
    probs = jnp.exp(score - new_top[:, :, None])
    total = jnp.sum(probs, axis=-1)
    update = jnp.einsum(
        "hqk,khe->hqe", probs.astype(jnp.bfloat16), value_heads, preferred_element_type=jnp.float32
    )
    return (new_top, total, update)


def body(tokens, slots, counts, shift, scale, gate, w_qkv, w_out):
    rows, width = tokens.shape
    nblk = rows // BLK
    heads = HEADS
    head_size = width // heads
    inverse = 1.0 / head_size**0.5
    onehot = slots.reshape(nblk, BLK)[:, :, None] == jnp.arange(BLK, dtype=jnp.int32)[None, None, :]
    sums = jnp.einsum(
        "bts,btd->bsd",
        onehot.astype(jnp.bfloat16),
        tokens.reshape(nblk, BLK, width),
        preferred_element_type=jnp.float32,
    )
    members = jnp.sum(onehot.astype(jnp.float32), axis=1)
    merged = (
        (sums / jnp.maximum(members, 1.0)[:, :, None]).astype(jnp.bfloat16).reshape(rows, width)
    )
    normed = layer_norm(merged, shift, scale)
    sizes = members.reshape(rows).astype(jnp.bfloat16)
    qkv = jnp.dot(normed, w_qkv, preferred_element_type=jnp.float32)
    query = qkv[:, :width].astype(jnp.bfloat16)
    keys = qkv[:, width : 2 * width].astype(jnp.bfloat16)
    values = qkv[:, 2 * width :].astype(jnp.bfloat16)
    alive = (
        (jnp.arange(BLK, dtype=jnp.int32)[None, :] < counts[:, None])
        .reshape(rows)
        .astype(jnp.bfloat16)
    )
    query_heads = query.reshape(rows, heads, head_size)
    keys_part = lax.all_gather(keys, "patch", axis=0, tiled=True)
    values_part = lax.all_gather(values, "patch", axis=0, tiled=True)
    sizes_part = lax.all_gather(sizes, "patch", axis=0, tiled=True)
    alive_part = lax.all_gather(alive, "patch", axis=0, tiled=True)
    bias = jnp.where(alive_part > 0, size_bias(sizes_part), -1e30)
    top, total, accum = attend_piece(
        query_heads, empty_carry(heads, rows, head_size), keys_part, values_part, bias, inverse
    )
    attended = finish(accum, total)
    projected = jnp.dot(attended, w_out, preferred_element_type=jnp.float32)
    branch = jnp.einsum(
        "bts,bsd->btd",
        onehot.astype(jnp.float32),
        projected.reshape(nblk, BLK, width),
        precision=lax.Precision.HIGHEST,
    ).reshape(rows, width)
    return (tokens.astype(jnp.float32) + gate * branch).astype(jnp.bfloat16)


def solution(mesh):
    return jax.shard_map(
        body,
        mesh=mesh,
        in_specs=(
            P(("batch", "patch"), None),
            P(("batch", "patch")),
            P(("batch", "patch")),
            P(),
            P(),
            P(),
            P(),
            P(),
        ),
        out_specs=P(("batch", "patch"), None),
        check_vma=False,
    )
```

profile of v0, /device:TPU:0, one launch (start us, length us, event | category | flops | bytes accessed | tf_op | source)
XLA Modules:
  0.0 205.7 jit_solution(10820672473933980348)
XLA Ops:
  6.5 0.0 copy-start
  6.5 0.0 all-gather.5.cloned.1.call-start
  6.5 0.9 convert_reduce_fusion
  7.5 1.4 fusion.27
  8.9 0.2 multiply_reduce_fusion
  9.1 0.7 broadcast_add_fusion
  9.8 4.7 %convolution_convert_fusion = bf16[128,3456]{1,0:T(8,128)(2,1)S(1)} fusion(bf16[1152,3456]{1,0:T(8,128)(2,1)} %param.14, f32[128,1152]{1,0:T(8,128)S(1)} %get-tuple-element.11, f32[1152]{0:T(1024)} %param.11, f32[1152]{0:T(1024)S(1)} %broadcast_add_fusion, f32[128]{0:T(128)S(1)} %add_rsqrt_fusion, f32[128]{0:T(128)S(1)} %broadcast_multiply_fusion), kind=kOutput, calls=%fused_computation.6 | convolution fusion | flops 1020395520 | bytes 9447424 | tf_op jit(solution)/shard_map/dot_general | solution.py:79
  14.5 0.9 fusion.26
  15.4 0.0 all-gather.5.cloned.1.call-update
  15.4 0.0 all-gather.7.cloned.1.call-start
  15.5 0.7 all-gather.7.cloned.1.call-update
  16.2 0.2 copy.18
  17.1 42.7 %all-gather.1 = bf16[16,1,128]{2,1,0:T(2,128)(2,1)S(1)} all-gather(bf16[1,1,128]{2,1,0:T(2,128)(2,1)S(1)} %get-tuple-element.8), channel_id=1, replica_groups=mesh['patch'=16,'batch'=2] {'patch'}, dimensions={0}, use_global_device_ids=true | all-gather | bytes 4352 | tf_op jit(solution)/shard_map/all_gather | solution.py:91
  59.7 36.4 %all-gather = bf16[16,1,128]{2,1,0:T(2,128)(2,1)S(1)} all-gather(bf16[1,1,128]{2,1,0:T(2,128)(2,1)S(1)} %fusion.24), channel_id=1, replica_groups=mesh['patch'=16,'batch'=2] {'patch'}, dimensions={0}, use_global_device_ids=true | all-gather | bytes 4352 | tf_op jit(solution)/shard_map/all_gather | solution.py:92
  96.1 2.0 all-gather.5.cloned.1.call-done
  98.1 6.7 %copy.19 = bf16[2048,1152]{0,1:T(8,128)(2,1)} copy(bf16[2048,1152]{1,0:T(8,128)(2,1)} %all-gather.5.cloned.1.call-done) | data formatting | bytes 9437184 | tf_op jit(solution)/shard_map/all_gather | solution.py:89
  104.9 4.5 %fusion = (f32[16,128]{1,0:T(8,128)S(1)}, f32[16,128,2048]{2,1,0:T(8,128)S(1)}) fusion(f32[2048]{0:T(1024)S(1)} %bitcast.30, bf16[128,16,72]{0,2,1:T(8,128)(2,1)S(1)} %bitcast.28, bf16[2048,16,72]{0,2,1:T(8,128)(2,1)} %bitcast.26), kind=kOutput, calls=%fused_computation.2 | convolution fusion | flops 616560640 | bytes 21807104 | tf_op jit(solution)/shard_map/qhe,khe->hqk/dot_general | solution.py:48
  109.3 0.0 copy-start.1
  109.4 5.7 %copy-done.1 = f32[16,128,2048]{2,1,0:T(8,128)} copy-done((f32[16,128,2048]{2,1,0:T(8,128)}, f32[16,128,2048]{2,1,0:T(8,128)S(1)}, u32[]{:S(2)}) %copy-start.1) | copy-done | bytes 16777240
  115.1 3.8 %fusion.1 = f32[16,128]{1,0:T(8,128)S(1)} fusion(f32[16,128,2048]{2,1,0:T(8,128)S(1)} %get-tuple-element.13, f32[16,128]{1,0:T(8,128)S(1)} %broadcast_maximum_fusion, f32[2048]{0:T(1024)S(1)} %bitcast.31), kind=kLoop, calls=%fused_computation.3 | loop fusion | flops 16775168 | bytes 16801792 | tf_op jit(solution)/shard_map/reduce_sum | solution.py:53
  118.8 60.6 %all-gather.7.cloned.1.call-done = bf16[2048,1152]{1,0:T(8,128)(2,1)} async-done(((bf16[128,1152]{1,0:T(8,128)(2,1)}), bf16[2048,1152]{1,0:T(8,128)(2,1)}) %all-gather.7.cloned.1.call-update) | async-done | bytes 4718608 | tf_op jit(solution)/shard_map/all_gather | solution.py:90
  179.4 6.7 %copy.20 = bf16[2048,1152]{0,1:T(8,128)(2,1)} copy(bf16[2048,1152]{1,0:T(8,128)(2,1)} %all-gather.7.cloned.1.call-done) | data formatting | bytes 9437184 | tf_op jit(solution)/shard_map/all_gather | solution.py:90
  186.1 0.0 copy-start.2
  186.1 0.0 copy-start.3
  186.1 0.0 copy-start.4
  186.1 10.9 %fusion.15 = bf16[128,16,72]{0,2,1:T(8,128)(2,1)S(1)} fusion(bf16[2048,16,72]{0,2,1:T(8,128)(2,1)} %bitcast.27, f32[16,128,2048]{2,1,0:T(8,128)} %copy-done.1, f32[16,128]{1,0:T(8,128)S(1)} %broadcast_maximum_fusion, f32[2048]{0:T(1024)S(1)} %bitcast.32, f32[128,16]{0,1:T(8,128)S(1)} %bitcast.33), kind=kOutput, calls=%fused_computation.15 | convolution fusion | flops 621051904 | bytes 21815296 | tf_op jit(solution)/shard_map/hqk,khe->hqe/dot_general | solution.py:54
  197.0 0.0 copy-done
  197.0 0.6 fusion.28
  197.6 0.0 copy-done.2
  197.6 0.0 copy-done.3
  197.7 0.0 copy-done.4
  197.7 1.2 fusion.8
  (6 shorter events, 0.1 us)
Async XLA Ops:
  6.5 190.5 %copy-start = (bf16[1152,1152]{1,0:T(8,128)(2,1)S(1)}, bf16[1152,1152]{1,0:T(8,128)(2,1)}, u32[]{:S(2)}) copy-start(bf16[1152,1152]{1,0:T(8,128)(2,1)} %param.15) | copy-start | bytes 7962628
  6.5 91.6 %all-gather.5.cloned.1.call-start = ((), (), s32[]{:S(2)}) async-start(), calls=%async_computation | async-start | bytes 5013504 | tf_op jit(solution)/shard_map/all_gather | solution.py:89
  15.4 163.9 %all-gather.7.cloned.1.call-start = ((), (), s32[]{:S(2)}) async-start(), calls=%async_computation.1 | async-start | bytes 5013504 | tf_op jit(solution)/shard_map/all_gather | solution.py:90
  109.3 5.7 %copy-start.1 = (f32[16,128,2048]{2,1,0:T(8,128)}, f32[16,128,2048]{2,1,0:T(8,128)S(1)}, u32[]{:S(2)}) copy-start(f32[16,128,2048]{2,1,0:T(8,128)S(1)} %get-tuple-element.13) | copy-start | bytes 50331652
  186.1 11.5 %copy-start.2 = (bf16[128,1152]{1,0:T(8,128)(2,1)S(1)}, bf16[128,1152]{1,0:T(8,128)(2,1)}, u32[]{:S(2)}) copy-start(bf16[128,1152]{1,0:T(8,128)(2,1)} %param.8) | copy-start | bytes 884740
  186.1 11.5 %copy-start.3 = (f32[1152]{0:T(1024)S(1)}, f32[1152]{0:T(1024)}, u32[]{:S(2)}) copy-start(f32[1152]{0:T(1024)} %param.13) | copy-start | bytes 13828
  186.1 11.5 %copy-start.4 = (s32[128]{0:T(128)S(1)}, s32[128]{0:T(128)}, u32[]{:S(2)}) copy-start(s32[128]{0:T(128)} %param.9) | copy-start | bytes 1540
Sparse Core Ops, SparseCore 0:
  15.6 82.5 all-gather.4
  100.9 78.4 all-gather.6
where the time goes:
time: 206 us
  blocking collectives  79 us (38%)
  waiting for transfers between devices  63.3 us (31%)
  matrix products  23.3 us (11%)
  local copies, waits for them, and re-layouts  20.3 us (10%)
  between operations  14.2 us (7%)
  other arithmetic  5.63 us (3%)
    all_gather x1, waiting for transfers between devices, body(): values_part = lax.all_gather(values, 'patch', axis=0, tiled=True)  60.6 us
    all_gather x1, blocking collectives, body(): sizes_part = lax.all_gather(sizes, 'patch', axis=0, tiled=True)  42.7 us
    all_gather x1, blocking collectives, body(): alive_part = lax.all_gather(alive, 'patch', axis=0, tiled=True)  36.4 us
    dot_general x1, matrix products, attend_piece(): jnp.einsum('hqk,khe->hqe', probs.astype(jnp.bfloat16), value_heads, prefe...  10.9 us
    all_gather x1, local copies, waits for them, and re-layouts, body(): values_part = lax.all_gather(values, 'patch', axis=0, tiled=True)  6.74 us
    all_gather x1, local copies, waits for them, and re-layouts, body(): keys_part = lax.all_gather(keys, 'patch', axis=0, tiled=True)  6.74 us
    unnamed x10, local copies, waits for them, and re-layouts  5.71 us
    dot_general x1, matrix products, body(): qkv = jnp.dot(normed, w_qkv, preferred_element_type=jnp.float32)  4.71 us
  transfers between devices with their start and end apart: 2, of which 2 were waited for; matrix products, arithmetic and copies ran while one was open for 7% of the time, Pallas kernels for 0%

commit v1 on v0

--- a/solution.py
+++ b/solution.py
@@ -87,7 +87,14 @@
     )
     query_heads = query.reshape(rows, heads, head_size)
     keys_part = lax.all_gather(keys, "patch", axis=0, tiled=True)
-    values_part = lax.all_gather(values, "patch", axis=0, tiled=True)
+    ring = [values]
+    for hop in range(15):
+        ring.append(lax.ppermute(ring[-1], "patch", [(dev, (dev + 1) % 16) for dev in range(16)]))
+    values_part = jnp.roll(
+        jnp.concatenate(ring[::-1], axis=0),
+        (lax.axis_index("patch") + 1) * ring[0].shape[0],
+        axis=0,
+    )
     sizes_part = lax.all_gather(sizes, "patch", axis=0, tiled=True)
     alive_part = lax.all_gather(alive, "patch", axis=0, tiled=True)
     bias = jnp.where(alive_part > 0, size_bias(sizes_part), -1e30)

time: 206 us -> 319 us (1.55)
  waiting for transfers between devices: 63.3 us -> 168 us
  local copies, waits for them, and re-layouts: 20.3 us -> 29.7 us
  blocking collectives: 79 us -> 74.6 us
    ppermute x0 -> x15, waiting for transfers between devices: none -> 168 us  [body(): lax.ppermute(ring[-1], 'patch', [(dev, (dev + 1) % 16) for dev in range(1...]
    all_gather x1 -> x0, waiting for transfers between devices: 60.6 us -> none  [body(): values_part = lax.all_gather(values, 'patch', axis=0, tiled=True)]
    dynamic_slice x0 -> x2, local copies, waits for them, and re-layouts: none -> 11.6 us  [body(): jnp.roll(jnp.concatenate(ring[::-1], axis=0), (lax.axis_index('patch') +...]
    all_gather x1, blocking collectives: 42.7 us -> 35.6 us  [body(): sizes_part = lax.all_gather(sizes, 'patch', axis=0, tiled=True)]
    all_gather x1 -> x0, local copies, waits for them, and re-layouts: 6.74 us -> none  [body(): values_part = lax.all_gather(values, 'patch', axis=0, tiled=True)]
    unnamed x10 -> x43, local copies, waits for them, and re-layouts: 5.71 us -> 10.4 us
  transfers between devices with their start and end apart: 2 -> 16, of which waited for: 2 -> 15; matrix products, arithmetic and copies ran while one was open for 7% -> 4% of each run, Pallas kernels for 0% -> 0%
where the time goes in v1:
time: 319 us
  waiting for transfers between devices  168 us (53%)
  blocking collectives  74.6 us (23%)
  local copies, waits for them, and re-layouts  29.7 us (9%)
  matrix products  23.3 us (7%)
  between operations  14.4 us (5%)
  other arithmetic  5.62 us (2%)
    ppermute x15, waiting for transfers between devices, body(): lax.ppermute(ring[-1], 'patch', [(dev, (dev + 1) % 16) for dev in range(1...  168 us
    all_gather x1, blocking collectives, body(): alive_part = lax.all_gather(alive, 'patch', axis=0, tiled=True)  39.1 us
    all_gather x1, blocking collectives, body(): sizes_part = lax.all_gather(sizes, 'patch', axis=0, tiled=True)  35.6 us
    dynamic_slice x2, local copies, waits for them, and re-layouts, body(): jnp.roll(jnp.concatenate(ring[::-1], axis=0), (lax.axis_index('patch') +...  11.6 us
    dot_general x1, matrix products, attend_piece(): jnp.einsum('hqk,khe->hqe', probs.astype(jnp.bfloat16), value_heads, prefe...  10.8 us
    unnamed x43, local copies, waits for them, and re-layouts  10.4 us
    all_gather x1, local copies, waits for them, and re-layouts, body(): keys_part = lax.all_gather(keys, 'patch', axis=0, tiled=True)  6.74 us
  transfers between devices with their start and end apart: 16, of which 15 were waited for; matrix products, arithmetic and copies ran while one was open for 4% of the time, Pallas kernels for 0%

profile of v1, /device:TPU:0, one launch (start us, length us, event | category | flops | bytes accessed | tf_op | source)
XLA Modules:
  0.0 318.6 jit_solution(2972510719511307166)
XLA Ops:
  6.5 0.9 convert_reduce_fusion
  7.5 0.7 broadcast_add_fusion
  8.2 1.4 fusion.27
  9.6 0.2 multiply_reduce_fusion
  9.8 4.7 %convolution_convert_fusion = bf16[128,3456]{1,0:T(8,128)(2,1)S(1)} fusion(bf16[1152,3456]{1,0:T(8,128)(2,1)} %param.14, f32[128,1152]{1,0:T(8,128)S(1)} %get-tuple-element.11, f32[1152]{0:T(1024)} %param.11, f32[1152]{0:T(1024)S(1)} %broadcast_add_fusion, f32[128]{0:T(128)S(1)} %add_rsqrt_fusion, f32[128]{0:T(128)S(1)} %broadcast_multiply_fusion), kind=kOutput, calls=%fused_computation.6 | convolution fusion | flops 1020395520 | bytes 9447424 | tf_op jit(solution)/shard_map/dot_general | solution.py:79
  14.6 3.0 collective-permute-start
  17.6 11.0 %collective-permute-done = bf16[128,1152]{1,0:T(8,128)(2,1)S(1)} collective-permute-done((bf16[128,1152]{1,0:T(8,128)(2,1)S(1)}, bf16[128,1152]{1,0:T(8,128)(2,1)S(1)}, u32[]{:S(2)}, u32[]{:S(2)}) %collective-permute-start) | collective-permute-done | bytes 294944 | tf_op jit(solution)/shard_map/ppermute | solution.py:92
  28.6 0.0 collective-permute-start.1
  28.6 11.8 %collective-permute-done.1 = bf16[128,1152]{1,0:T(8,128)(2,1)S(1)} collective-permute-done((bf16[128,1152]{1,0:T(8,128)(2,1)S(1)}, bf16[128,1152]{1,0:T(8,128)(2,1)S(1)}, u32[]{:S(2)}, u32[]{:S(2)}) %collective-permute-start.1) | collective-permute-done | bytes 294944 | tf_op jit(solution)/shard_map/ppermute | solution.py:92
  40.4 0.0 collective-permute-start.2
  40.4 10.9 %collective-permute-done.2 = bf16[128,1152]{1,0:T(8,128)(2,1)S(1)} collective-permute-done((bf16[128,1152]{1,0:T(8,128)(2,1)S(1)}, bf16[128,1152]{1,0:T(8,128)(2,1)S(1)}, u32[]{:S(2)}, u32[]{:S(2)}) %collective-permute-start.2) | collective-permute-done | bytes 294944 | tf_op jit(solution)/shard_map/ppermute | solution.py:92
  51.3 0.0 collective-permute-start.3
  51.3 10.3 %collective-permute-done.3 = bf16[128,1152]{1,0:T(8,128)(2,1)S(1)} collective-permute-done((bf16[128,1152]{1,0:T(8,128)(2,1)S(1)}, bf16[128,1152]{1,0:T(8,128)(2,1)S(1)}, u32[]{:S(2)}, u32[]{:S(2)}) %collective-permute-start.3) | collective-permute-done | bytes 294944 | tf_op jit(solution)/shard_map/ppermute | solution.py:92
  61.6 0.0 collective-permute-start.4
  61.6 10.3 %collective-permute-done.4 = bf16[128,1152]{1,0:T(8,128)(2,1)S(1)} collective-permute-done((bf16[128,1152]{1,0:T(8,128)(2,1)S(1)}, bf16[128,1152]{1,0:T(8,128)(2,1)S(1)}, u32[]{:S(2)}, u32[]{:S(2)}) %collective-permute-start.4) | collective-permute-done | bytes 294944 | tf_op jit(solution)/shard_map/ppermute | solution.py:92
  71.9 0.0 collective-permute-start.5
  71.9 10.3 %collective-permute-done.5 = bf16[128,1152]{1,0:T(8,128)(2,1)S(1)} collective-permute-done((bf16[128,1152]{1,0:T(8,128)(2,1)S(1)}, bf16[128,1152]{1,0:T(8,128)(2,1)S(1)}, u32[]{:S(2)}, u32[]{:S(2)}) %collective-permute-start.5) | collective-permute-done | bytes 294944 | tf_op jit(solution)/shard_map/ppermute | solution.py:92
  82.2 0.0 collective-permute-start.6
  82.2 11.2 %collective-permute-done.6 = bf16[128,1152]{1,0:T(8,128)(2,1)S(1)} collective-permute-done((bf16[128,1152]{1,0:T(8,128)(2,1)S(1)}, bf16[128,1152]{1,0:T(8,128)(2,1)S(1)}, u32[]{:S(2)}, u32[]{:S(2)}) %collective-permute-start.6) | collective-permute-done | bytes 294944 | tf_op jit(solution)/shard_map/ppermute | solution.py:92
  93.4 0.0 collective-permute-start.7
  93.4 12.3 %collective-permute-done.7 = bf16[128,1152]{1,0:T(8,128)(2,1)S(1)} collective-permute-done((bf16[128,1152]{1,0:T(8,128)(2,1)S(1)}, bf16[128,1152]{1,0:T(8,128)(2,1)S(1)}, u32[]{:S(2)}, u32[]{:S(2)}) %collective-permute-start.7) | collective-permute-done | bytes 294944 | tf_op jit(solution)/shard_map/ppermute | solution.py:92
  105.7 13.5 %collective-permute-done.8 = bf16[128,1152]{1,0:T(8,128)(2,1)S(1)} collective-permute-done((bf16[128,1152]{1,0:T(8,128)(2,1)S(1)}, bf16[128,1152]{1,0:T(8,128)(2,1)S(1)}, u32[]{:S(2)}, u32[]{:S(2)}) %collective-permute-start.8) | collective-permute-done | bytes 294944 | tf_op jit(solution)/shard_map/ppermute | solution.py:92
  119.2 12.6 %collective-permute-done.9 = bf16[128,1152]{1,0:T(8,128)(2,1)S(1)} collective-permute-done((bf16[128,1152]{1,0:T(8,128)(2,1)S(1)}, bf16[128,1152]{1,0:T(8,128)(2,1)S(1)}, u32[]{:S(2)}, u32[]{:S(2)}) %collective-permute-start.9) | collective-permute-done | bytes 294944 | tf_op jit(solution)/shard_map/ppermute | solution.py:92
  131.8 0.0 collective-permute-start.10
  131.8 11.8 %collective-permute-done.10 = bf16[128,1152]{1,0:T(8,128)(2,1)S(1)} collective-permute-done((bf16[128,1152]{1,0:T(8,128)(2,1)S(1)}, bf16[128,1152]{1,0:T(8,128)(2,1)S(1)}, u32[]{:S(2)}, u32[]{:S(2)}) %collective-permute-start.10) | collective-permute-done | bytes 294944 | tf_op jit(solution)/shard_map/ppermute | solution.py:92
  143.6 10.9 %collective-permute-done.11 = bf16[128,1152]{1,0:T(8,128)(2,1)S(1)} collective-permute-done((bf16[128,1152]{1,0:T(8,128)(2,1)S(1)}, bf16[128,1152]{1,0:T(8,128)(2,1)S(1)}, u32[]{:S(2)}, u32[]{:S(2)}) %collective-permute-start.11) | collective-permute-done | bytes 294944 | tf_op jit(solution)/shard_map/ppermute | solution.py:92
  154.5 10.3 %collective-permute-done.12 = bf16[128,1152]{1,0:T(8,128)(2,1)S(1)} collective-permute-done((bf16[128,1152]{1,0:T(8,128)(2,1)S(1)}, bf16[128,1152]{1,0:T(8,128)(2,1)S(1)}, u32[]{:S(2)}, u32[]{:S(2)}) %collective-permute-start.12) | collective-permute-done | bytes 294944 | tf_op jit(solution)/shard_map/ppermute | solution.py:92
  164.8 0.0 collective-permute-start.13
  164.8 10.3 %collective-permute-done.13 = bf16[128,1152]{1,0:T(8,128)(2,1)S(1)} collective-permute-done((bf16[128,1152]{1,0:T(8,128)(2,1)S(1)}, bf16[128,1152]{1,0:T(8,128)(2,1)S(1)}, u32[]{:S(2)}, u32[]{:S(2)}) %collective-permute-start.13) | collective-permute-done | bytes 294944 | tf_op jit(solution)/shard_map/ppermute | solution.py:92
  175.2 10.3 %collective-permute-done.14 = bf16[128,1152]{1,0:T(8,128)(2,1)S(1)} collective-permute-done((bf16[128,1152]{1,0:T(8,128)(2,1)S(1)}, bf16[128,1152]{1,0:T(8,128)(2,1)S(1)}, u32[]{:S(2)}, u32[]{:S(2)}) %collective-permute-start.14) | collective-permute-done | bytes 294944 | tf_op jit(solution)/shard_map/ppermute | solution.py:92
  186.7 0.8 fusion.26
  187.5 3.6 %copy-done.2 = bf16[4096,1152]{1,0:T(8,128)(2,1)} copy-done((bf16[4096,1152]{1,0:T(8,128)(2,1)}, bf16[4096,1152]{1,0:T(8,128)(2,1)S(1)}, u32[]{:S(2)}) %copy-start.2) | copy-done | bytes 9437208
  191.1 0.0 all-gather.4.cloned.1.call-update
  191.8 35.6 %all-gather.1 = bf16[16,1,128]{2,1,0:T(2,128)(2,1)S(1)} all-gather(bf16[1,1,128]{2,1,0:T(2,128)(2,1)S(1)} %get-tuple-element.8), channel_id=1, replica_groups=mesh['patch'=16,'batch'=2] {'patch'}, dimensions={0}, use_global_device_ids=true | all-gather | bytes 4352 | tf_op jit(solution)/shard_map/all_gather | solution.py:98
  227.4 39.1 %all-gather = bf16[16,1,128]{2,1,0:T(2,128)(2,1)S(1)} all-gather(bf16[1,1,128]{2,1,0:T(2,128)(2,1)S(1)} %fusion.24), channel_id=1, replica_groups=mesh['patch'=16,'batch'=2] {'patch'}, dimensions={0}, use_global_device_ids=true | all-gather | bytes 4352 | tf_op jit(solution)/shard_map/all_gather | solution.py:99
  266.5 0.2 copy.17
  266.7 4.9 %constant_dynamic-slice_fusion = bf16[2048,1152]{1,0:T(8,128)(2,1)} fusion(bf16[4096,1152]{1,0:T(8,128)(2,1)} %copy-done.2, s32[]{:T(128)S(6)} %select_n.19), kind=kLoop, calls=%fused_computation.66 | loop fusion | bytes 9437188 | tf_op jit(solution)/shard_map/jit(_roll_dynamic)/dynamic_slice | solution.py:93
  271.6 6.7 %copy.19 = bf16[2048,1152]{0,1:T(8,128)(2,1)} copy(bf16[2048,1152]{1,0:T(8,128)(2,1)} %constant_dynamic-slice_fusion) | data formatting | bytes 9437184 | tf_op jit(solution)/shard_map/jit(_roll_dynamic)/dynamic_slice | solution.py:93
  278.3 6.7 %copy.18 = bf16[2048,1152]{0,1:T(8,128)(2,1)} copy(bf16[2048,1152]{1,0:T(8,128)(2,1)} %all-gather.4.cloned.1.call-done) | data formatting | bytes 9437184 | tf_op jit(solution)/shard_map/all_gather | solution.py:89
  285.0 4.5 %fusion = (f32[16,128]{1,0:T(8,128)S(1)}, f32[16,128,2048]{2,1,0:T(8,128)S(1)}) fusion(f32[2048]{0:T(1024)S(1)} %bitcast.30, bf16[128,16,72]{0,2,1:T(8,128)(2,1)S(1)} %bitcast.28, bf16[2048,16,72]{0,2,1:T(8,128)(2,1)} %bitcast.26), kind=kOutput, calls=%fused_computation.2 | convolution fusion | flops 616560640 | bytes 21807104 | tf_op jit(solution)/shard_map/qhe,khe->hqk/dot_general | solution.py:48
  289.6 5.7 %copy-done.1 = f32[16,128,2048]{2,1,0:T(8,128)} copy-done((f32[16,128,2048]{2,1,0:T(8,128)}, f32[16,128,2048]{2,1,0:T(8,128)S(1)}, u32[]{:S(2)}) %copy-start.1) | copy-done | bytes 16777240
  295.3 3.8 %fusion.1 = f32[16,128]{1,0:T(8,128)S(1)} fusion(f32[16,128,2048]{2,1,0:T(8,128)S(1)} %get-tuple-element.13, f32[16,128]{1,0:T(8,128)S(1)} %broadcast_maximum_fusion, f32[2048]{0:T(1024)S(1)} %bitcast.31), kind=kLoop, calls=%fused_computation.3 | loop fusion | flops 16775168 | bytes 16801792 | tf_op jit(solution)/shard_map/reduce_sum | solution.py:53
  299.0 0.0 copy-start.3
  299.0 0.0 copy-start.4
  299.1 0.0 copy-start.5
  299.1 10.8 %fusion.15 = bf16[128,16,72]{0,2,1:T(8,128)(2,1)S(1)} fusion(bf16[2048,16,72]{0,2,1:T(8,128)(2,1)} %bitcast.27, f32[16,128,2048]{2,1,0:T(8,128)} %copy-done.1, f32[16,128]{1,0:T(8,128)S(1)} %broadcast_maximum_fusion, f32[2048]{0:T(1024)S(1)} %bitcast.32, f32[128,16]{0,1:T(8,128)S(1)} %bitcast.33), kind=kOutput, calls=%fused_computation.15 | convolution fusion | flops 621051904 | bytes 21815296 | tf_op jit(solution)/shard_map/hqk,khe->hqe/dot_general | solution.py:54
  309.9 0.6 fusion.28
  310.6 1.2 fusion.8
  (52 shorter events, 1.1 us)
Async XLA Ops:
  6.5 303.4 %copy-start = (bf16[1152,1152]{1,0:T(8,128)(2,1)S(1)}, bf16[1152,1152]{1,0:T(8,128)(2,1)}, u32[]{:S(2)}) copy-start(bf16[1152,1152]{1,0:T(8,128)(2,1)} %param.15) | copy-start | bytes 7962628
  6.5 271.8 %all-gather.4.cloned.1.call-start = ((), (), s32[]{:S(2)}) async-start(), calls=%async_computation | async-start | bytes 5013504 | tf_op jit(solution)/shard_map/all_gather | solution.py:89
  14.6 14.0 %collective-permute-start = (bf16[128,1152]{1,0:T(8,128)(2,1)S(1)}, bf16[128,1152]{1,0:T(8,128)(2,1)S(1)}, u32[]{:S(2)}, u32[]{:S(2)}) collective-permute-start(bf16[128,1152]{1,0:T(8,128)(2,1)S(1)} %slice.17), channel_id=1, source_target_pairs={{0,2},{2,4},{4,6},{6,8},{8,10},{10,12},{12,14},{14,16},{16,18},{18... | collective-permute-start | bytes 884744 | tf_op jit(solution)/shard_map/ppermute | solution.py:92
  28.6 11.8 %collective-permute-start.1 = (bf16[128,1152]{1,0:T(8,128)(2,1)S(1)}, bf16[128,1152]{1,0:T(8,128)(2,1)S(1)}, u32[]{:S(2)}, u32[]{:S(2)}) collective-permute-start(bf16[128,1152]{1,0:T(8,128)(2,1)S(1)} %collective-permute-done), channel_id=1, source_target_pairs={{0,2},{2,4},{4,6},{6,8},{8,10},{10,12},{12,14},{14,16},{16,18},{18... | collective-permute-start | bytes 884744 | tf_op jit(solution)/shard_map/ppermute | solution.py:92
  40.4 10.9 %collective-permute-start.2 = (bf16[128,1152]{1,0:T(8,128)(2,1)S(1)}, bf16[128,1152]{1,0:T(8,128)(2,1)S(1)}, u32[]{:S(2)}, u32[]{:S(2)}) collective-permute-start(bf16[128,1152]{1,0:T(8,128)(2,1)S(1)} %collective-permute-done.1), channel_id=1, source_target_pairs={{0,2},{2,4},{4,6},{6,8},{8,10},{10,12},{12,14},{14,16},{16,18},{18... | collective-permute-start | bytes 884744 | tf_op jit(solution)/shard_map/ppermute | solution.py:92
  51.3 10.3 %collective-permute-start.3 = (bf16[128,1152]{1,0:T(8,128)(2,1)S(1)}, bf16[128,1152]{1,0:T(8,128)(2,1)S(1)}, u32[]{:S(2)}, u32[]{:S(2)}) collective-permute-start(bf16[128,1152]{1,0:T(8,128)(2,1)S(1)} %collective-permute-done.2), channel_id=1, source_target_pairs={{0,2},{2,4},{4,6},{6,8},{8,10},{10,12},{12,14},{14,16},{16,18},{18... | collective-permute-start | bytes 884744 | tf_op jit(solution)/shard_map/ppermute | solution.py:92
  61.6 10.3 %collective-permute-start.4 = (bf16[128,1152]{1,0:T(8,128)(2,1)S(1)}, bf16[128,1152]{1,0:T(8,128)(2,1)S(1)}, u32[]{:S(2)}, u32[]{:S(2)}) collective-permute-start(bf16[128,1152]{1,0:T(8,128)(2,1)S(1)} %collective-permute-done.3), channel_id=1, source_target_pairs={{0,2},{2,4},{4,6},{6,8},{8,10},{10,12},{12,14},{14,16},{16,18},{18... | collective-permute-start | bytes 884744 | tf_op jit(solution)/shard_map/ppermute | solution.py:92
  71.9 10.3 %collective-permute-start.5 = (bf16[128,1152]{1,0:T(8,128)(2,1)S(1)}, bf16[128,1152]{1,0:T(8,128)(2,1)S(1)}, u32[]{:S(2)}, u32[]{:S(2)}) collective-permute-start(bf16[128,1152]{1,0:T(8,128)(2,1)S(1)} %collective-permute-done.4), channel_id=1, source_target_pairs={{0,2},{2,4},{4,6},{6,8},{8,10},{10,12},{12,14},{14,16},{16,18},{18... | collective-permute-start | bytes 884744 | tf_op jit(solution)/shard_map/ppermute | solution.py:92
  82.2 11.2 %collective-permute-start.6 = (bf16[128,1152]{1,0:T(8,128)(2,1)S(1)}, bf16[128,1152]{1,0:T(8,128)(2,1)S(1)}, u32[]{:S(2)}, u32[]{:S(2)}) collective-permute-start(bf16[128,1152]{1,0:T(8,128)(2,1)S(1)} %collective-permute-done.5), channel_id=1, source_target_pairs={{0,2},{2,4},{4,6},{6,8},{8,10},{10,12},{12,14},{14,16},{16,18},{18... | collective-permute-start | bytes 884744 | tf_op jit(solution)/shard_map/ppermute | solution.py:92
  93.4 12.3 %collective-permute-start.7 = (bf16[128,1152]{1,0:T(8,128)(2,1)S(1)}, bf16[128,1152]{1,0:T(8,128)(2,1)S(1)}, u32[]{:S(2)}, u32[]{:S(2)}) collective-permute-start(bf16[128,1152]{1,0:T(8,128)(2,1)S(1)} %collective-permute-done.6), channel_id=1, source_target_pairs={{0,2},{2,4},{4,6},{6,8},{8,10},{10,12},{12,14},{14,16},{16,18},{18... | collective-permute-start | bytes 884744 | tf_op jit(solution)/shard_map/ppermute | solution.py:92
  105.7 13.5 %collective-permute-start.8 = (bf16[128,1152]{1,0:T(8,128)(2,1)S(1)}, bf16[128,1152]{1,0:T(8,128)(2,1)S(1)}, u32[]{:S(2)}, u32[]{:S(2)}) collective-permute-start(bf16[128,1152]{1,0:T(8,128)(2,1)S(1)} %collective-permute-done.7), channel_id=1, source_target_pairs={{0,2},{2,4},{4,6},{6,8},{8,10},{10,12},{12,14},{14,16},{16,18},{18... | collective-permute-start | bytes 884744 | tf_op jit(solution)/shard_map/ppermute | solution.py:92
  119.2 12.6 %collective-permute-start.9 = (bf16[128,1152]{1,0:T(8,128)(2,1)S(1)}, bf16[128,1152]{1,0:T(8,128)(2,1)S(1)}, u32[]{:S(2)}, u32[]{:S(2)}) collective-permute-start(bf16[128,1152]{1,0:T(8,128)(2,1)S(1)} %collective-permute-done.8), channel_id=1, source_target_pairs={{0,2},{2,4},{4,6},{6,8},{8,10},{10,12},{12,14},{14,16},{16,18},{18... | collective-permute-start | bytes 884744 | tf_op jit(solution)/shard_map/ppermute | solution.py:92
  131.8 11.8 %collective-permute-start.10 = (bf16[128,1152]{1,0:T(8,128)(2,1)S(1)}, bf16[128,1152]{1,0:T(8,128)(2,1)S(1)}, u32[]{:S(2)}, u32[]{:S(2)}) collective-permute-start(bf16[128,1152]{1,0:T(8,128)(2,1)S(1)} %collective-permute-done.9), channel_id=1, source_target_pairs={{0,2},{2,4},{4,6},{6,8},{8,10},{10,12},{12,14},{14,16},{16,18},{18... | collective-permute-start | bytes 884744 | tf_op jit(solution)/shard_map/ppermute | solution.py:92
  143.6 10.9 %collective-permute-start.11 = (bf16[128,1152]{1,0:T(8,128)(2,1)S(1)}, bf16[128,1152]{1,0:T(8,128)(2,1)S(1)}, u32[]{:S(2)}, u32[]{:S(2)}) collective-permute-start(bf16[128,1152]{1,0:T(8,128)(2,1)S(1)} %collective-permute-done.10), channel_id=1, source_target_pairs={{0,2},{2,4},{4,6},{6,8},{8,10},{10,12},{12,14},{14,16},{16,18},{18... | collective-permute-start | bytes 884744 | tf_op jit(solution)/shard_map/ppermute | solution.py:92
  154.5 10.3 %collective-permute-start.12 = (bf16[128,1152]{1,0:T(8,128)(2,1)S(1)}, bf16[128,1152]{1,0:T(8,128)(2,1)S(1)}, u32[]{:S(2)}, u32[]{:S(2)}) collective-permute-start(bf16[128,1152]{1,0:T(8,128)(2,1)S(1)} %collective-permute-done.11), channel_id=1, source_target_pairs={{0,2},{2,4},{4,6},{6,8},{8,10},{10,12},{12,14},{14,16},{16,18},{18... | collective-permute-start | bytes 884744 | tf_op jit(solution)/shard_map/ppermute | solution.py:92
  164.8 10.3 %collective-permute-start.13 = (bf16[128,1152]{1,0:T(8,128)(2,1)S(1)}, bf16[128,1152]{1,0:T(8,128)(2,1)S(1)}, u32[]{:S(2)}, u32[]{:S(2)}) collective-permute-start(bf16[128,1152]{1,0:T(8,128)(2,1)S(1)} %collective-permute-done.12), channel_id=1, source_target_pairs={{0,2},{2,4},{4,6},{6,8},{8,10},{10,12},{12,14},{14,16},{16,18},{18... | collective-permute-start | bytes 884744 | tf_op jit(solution)/shard_map/ppermute | solution.py:92
  175.2 10.3 %collective-permute-start.14 = (bf16[128,1152]{1,0:T(8,128)(2,1)S(1)}, bf16[128,1152]{1,0:T(8,128)(2,1)S(1)}, u32[]{:S(2)}, u32[]{:S(2)}) collective-permute-start(bf16[128,1152]{1,0:T(8,128)(2,1)S(1)} %collective-permute-done.13), channel_id=1, source_target_pairs={{0,2},{2,4},{4,6},{6,8},{8,10},{10,12},{12,14},{14,16},{16,18},{18... | collective-permute-start | bytes 884744 | tf_op jit(solution)/shard_map/ppermute | solution.py:92
  187.5 3.6 %copy-start.2 = (bf16[4096,1152]{1,0:T(8,128)(2,1)}, bf16[4096,1152]{1,0:T(8,128)(2,1)S(1)}, u32[]{:S(2)}) copy-start(bf16[4096,1152]{1,0:T(8,128)(2,1)S(1)} %get-tuple-element.6) | copy-start | bytes 28311556
  289.5 5.7 %copy-start.1 = (f32[16,128,2048]{2,1,0:T(8,128)}, f32[16,128,2048]{2,1,0:T(8,128)S(1)}, u32[]{:S(2)}) copy-start(f32[16,128,2048]{2,1,0:T(8,128)S(1)} %get-tuple-element.13) | copy-start | bytes 50331652
  299.0 11.5 %copy-start.3 = (bf16[128,1152]{1,0:T(8,128)(2,1)S(1)}, bf16[128,1152]{1,0:T(8,128)(2,1)}, u32[]{:S(2)}) copy-start(bf16[128,1152]{1,0:T(8,128)(2,1)} %param.8) | copy-start | bytes 884740
  299.0 11.5 %copy-start.4 = (f32[1152]{0:T(1024)S(1)}, f32[1152]{0:T(1024)}, u32[]{:S(2)}) copy-start(f32[1152]{0:T(1024)} %param.13) | copy-start | bytes 13828
  299.1 11.5 %copy-start.5 = (s32[128]{0:T(128)S(1)}, s32[128]{0:T(128)}, u32[]{:S(2)}) copy-start(s32[128]{0:T(128)} %param.9) | copy-start | bytes 1540
Sparse Core Ops, SparseCore 0:
  191.3 75.6 all-gather.3
